TPU v7x, 256 devices: a whole 4x4x8 slice. The times are simulated.
256 devices in a mesh: section: 16 (over y, z_lo, core), dp: 4 (over x), mp: 4 (over z_hi).
Axes of the slice: x: 4, y: 4, z: 8 (z_hi: 4, z_lo: 2; z = z_hi * 2 + z_lo), core: 2. Of those that a mesh axis runs over, the one named last changes fastest.
Arguments:
- patches: bfloat16 [32768, 1280], P(('section', 'dp')), may hold values from -6 to 6
- patch_counts: int32 [128], P(('section', 'dp')), may hold values from 8 to 256, as said below
- dest_rows: int32 [8192], P(('section', 'dp')), may hold values from 0 to 32767, as said below
- qkv_weight: bfloat16 [1280, 3, 1280], P(None, None, 'mp'), may hold values from -1 to 1
- out_weight: bfloat16 [1280, 1280], P('mp'), may hold values from -0.15625 to 0.15625
- attn_gain: bfloat16 [1280], replicated, may hold values from 0.25 to 1.75
- merge_gain: bfloat16 [1280], replicated, may hold values from 0.25 to 1.75
- fc1_weight: bfloat16 [5120, 5120], P('mp', ('section', 'dp')), may hold values from -0.078125 to 0.078125
- fc1_bias: bfloat16 [5120], P(('section', 'dp')), may hold values from -3 to 3
- fc2_weight: bfloat16 [5120, 8192], P(('section', 'dp'), 'mp'), may hold values from -0.078125 to 0.078125
- fc2_bias: bfloat16 [8192], P('mp'), may hold values from -3 to 3
- text_embeds: bfloat16 [32768, 8192], P(('section', 'dp'), 'mp'), may hold values from -6 to 6
- section_hidden: bfloat16 [32768, 8192], P(('section', 'dp'), 'mp'), may hold values from -80 to 80
- llm_gain: bfloat16 [8192], P('mp'), may hold values from 0.25 to 1.75
Outputs:
- sequence_embeds: bfloat16 [32768, 8192], P(('section', 'dp'), 'mp')
- layer_inputs: bfloat16 [32768, 8192], P(('section', 'dp'), 'mp')
Inputs may be any that keep to these rules, and one draw needn't show every extreme that they name: `patch_counts`: multiples of 4; a tile's patches fill the first slots of its block. `dest_rows`: all rows differ. Each group's merged slots form runs of 2 consecutive slots (aligned); a run goes to one sequence slice (row // 512, numbered in section-major order), different runs of a group to different slices. Rows of slots that are not live are never written.
All inputs are finite; a program needn't handle non-finite values.
Results may differ from a plain program's by a relative error of at most 0.0055.
Values may be sent and summed in bfloat16 or wider, within the bound.
A program may use at most 128 MiB of HBM per device.

v0:
```python
import jax
import jax.numpy as jnp
from jax import lax
from jax.sharding import PartitionSpec as P

HEAD_DIM = 80
HID = 8192
vit_eps = 1e-06
llm_eps = 1e-06


def gather_turned(arrays, axis, dims):
    turned = [jnp.moveaxis(a, dim, 0) for a, dim in zip(arrays, dims)]
    widths = [t[0].size for t in turned]
    both = jnp.concatenate([t.reshape(-1, w) for t, w in zip(turned, widths)], axis=1)
    out = lax.all_gather(both, axis, axis=0, tiled=True)
    blocks = jnp.split(out, [sum(widths[:k]) for k in range(1, len(widths))], axis=1)
    return tuple(
        (
            jnp.moveaxis(b.reshape(-1, *t.shape[1:]), 0, dim)
            for b, t, dim in zip(blocks, turned, dims)
        )
    )


def joined_along(blocks, dim):
    blocks = jnp.moveaxis(blocks, 0, dim)
    shape = blocks.shape
    return blocks.reshape(*shape[:dim], shape[dim] * shape[dim + 1], *shape[dim + 2 :])


def copy_for_each(value, axis):
    copies = jnp.broadcast_to(value, (lax.axis_size(axis), *value.shape))
    return lax.all_to_all(copies, axis, split_axis=0, concat_axis=0, tiled=True)


def gathered_copies(value, axis, dim):
    return joined_along(copy_for_each(value, axis), dim)


def cut_along(value, dim, devices):
    before, after = (value.shape[:dim], value.shape[dim + 1 :])
    return jnp.moveaxis(value.reshape(*before, devices, -1, *after), dim, 0)


def sent_and_summed(value, axis, dim):
    devices = lax.axis_size(axis)
    blocks = lax.all_to_all(cut_along(value, dim, devices), axis, 0, 0, tiled=True)
    return jnp.sum(blocks.astype(jnp.float32), axis=0)


def from_behind(value, axis, steps):
    count = lax.axis_size(axis)
    first, last = (max(0, -steps), min(count, count - steps))
    return lax.ppermute(value, axis, [(source, source + steps) for source in range(first, last)])


def over_copies(value, axis):
    return copy_for_each(value, axis).sum(axis=0)


def layer_norm(values, gain):
    centred = values.astype(jnp.float32)
    centred = centred - jnp.mean(centred, axis=-1, keepdims=True)
    variance = jnp.mean(centred * centred, axis=-1, keepdims=True)
    return centred * lax.rsqrt(variance + vit_eps) * gain.astype(jnp.float32)


def per_device(
    patches,
    patch_counts,
    dest_rows,
    qkv_weight,
    out_weight,
    attn_gain,
    merge_gain,
    fc1_weight,
    fc1_bias,
    fc2_weight,
    fc2_bias,
    text_embeds,
    section_hidden,
    llm_gain,
):
    width = patches.shape[1]
    tile_total = patch_counts.shape[0]
    block_rows = patches.shape[0] // tile_total
    merged_rows = patches.shape[0] // 4
    local_cols = qkv_weight.shape[2]
    local_heads = local_cols // HEAD_DIM
    feature_cols = text_embeds.shape[1]
    seq_rows = text_embeds.shape[0]
    section_count = lax.axis_size("section")
    group_count = section_count * lax.axis_size("dp")
    run_cap = max(2, merged_rows // group_count)
    run_total = merged_rows // run_cap
    normed_in = layer_norm(patches, attn_gain).astype(jnp.bfloat16)
    projections = jnp.dot(
        normed_in, qkv_weight.reshape(width, 3 * local_cols), preferred_element_type=jnp.float32
    ).astype(jnp.bfloat16)
    projections = projections.reshape(tile_total, block_rows, 3, local_heads, HEAD_DIM)
    query_part = projections[:, :, 0]
    key_part = projections[:, :, 1]
    value_part = projections[:, :, 2]
    scores = jnp.einsum(
        "tqhd,tkhd->thqk", query_part, key_part, preferred_element_type=jnp.float32
    ) * HEAD_DIM ** (-0.5)
    key_live = (
        jnp.arange(block_rows, dtype=jnp.int32)[None, None, None, :]
        < patch_counts[:, None, None, None]
    )
    scores = jnp.where(key_live, scores, -1e30)
    weights = jax.nn.softmax(scores, axis=-1).astype(jnp.bfloat16)
    attended = jnp.einsum(
        "thqk,tkhd->tqhd", weights, value_part, preferred_element_type=jnp.float32
    ).astype(jnp.bfloat16)
    attended = attended.reshape(patches.shape[0], local_cols)
    partial_proj = jnp.dot(attended, out_weight, preferred_element_type=jnp.float32)
    position = lax.axis_index("mp")
    own_patch = lax.dynamic_slice_in_dim(
        patches.reshape(merged_rows, 4, width), position, 1, 1
    ).reshape(merged_rows, width)
    own_proj = lax.psum_scatter(
        partial_proj.reshape(merged_rows, 4, width), "mp", scatter_dimension=1, tiled=True
    ).reshape(merged_rows, width)
    block_out = (own_patch.astype(jnp.float32) + own_proj).astype(jnp.bfloat16)
    merge_part = layer_norm(block_out, merge_gain).astype(jnp.bfloat16)
    first_full, second_full, bias_full = gather_turned(
        (fc1_weight, fc2_weight, fc1_bias), "section", (1, 0, 0)
    )
    first_partial = jnp.dot(
        gathered_copies(merge_part, "dp", 0), first_full, preferred_element_type=jnp.float32
    )
    first_total = lax.psum(first_partial.astype(jnp.bfloat16), "mp").astype(jnp.float32)
    hidden = jax.nn.gelu(first_total + bias_full.astype(jnp.float32), approximate=False).astype(
        jnp.bfloat16
    )
    embed_total = sent_and_summed(
        jnp.dot(hidden, second_full, preferred_element_type=jnp.float32).astype(jnp.bfloat16),
        "dp",
        0,
    )
    image_embeds = (embed_total + fc2_bias.astype(jnp.float32)).astype(jnp.bfloat16)
    slot_in_tile = jnp.arange(merged_rows, dtype=jnp.int32) % (block_rows // 4)
    tile_counts = jnp.repeat(patch_counts, block_rows // 4, total_repeat_length=merged_rows)
    live = slot_in_tile * 4 < tile_counts
    receiver = dest_rows // seq_rows
    run_target = receiver.reshape(run_total, run_cap)[:, 0]
    place = jnp.where(live, dest_rows % seq_rows, seq_rows)
    send_rows = (
        jnp.zeros((group_count, run_cap, feature_cols), jnp.bfloat16)
        .at[run_target]
        .set(image_embeds.reshape(run_total, run_cap, feature_cols))
    )
    send_place = (
        jnp.full((group_count, run_cap), seq_rows, jnp.int32)
        .at[run_target]
        .set(place.reshape(run_total, run_cap))
    )
    got_rows, got_place = (
        lax.all_to_all(send_rows, ("section", "dp"), split_axis=0, concat_axis=0, tiled=True),
        lax.all_to_all(send_place, ("section", "dp"), split_axis=0, concat_axis=0, tiled=True),
    )
    sequence_embeds = text_embeds.at[got_place.reshape(-1)].set(
        got_rows.reshape(-1, feature_cols), mode="drop"
    )
    incoming = from_behind(section_hidden, "section", 1)
    entering = jnp.where(lax.axis_index("section") == 0, sequence_embeds, incoming).astype(
        jnp.float32
    )
    row_total = over_copies(jnp.sum(entering * entering, axis=1), "mp")
    layer_inputs = (
        entering * lax.rsqrt(row_total / HID + llm_eps)[:, None] * llm_gain.astype(jnp.float32)
    ).astype(jnp.bfloat16)
    return (sequence_embeds, layer_inputs)


def solution(mesh):
    in_specs = (
        P(("section", "dp"), None),
        P(("section", "dp")),
        P(("section", "dp")),
        P(None, None, "mp"),
        P("mp", None),
        P(),
        P(),
        P("mp", ("section", "dp")),
        P(("section", "dp")),
        P(("section", "dp"), "mp"),
        P("mp"),
        P(("section", "dp"), "mp"),
        P(("section", "dp"), "mp"),
        P("mp"),
    )
    out_specs = (P(("section", "dp"), "mp"), P(("section", "dp"), "mp"))
    return jax.shard_map(
        per_device, mesh=mesh, in_specs=in_specs, out_specs=out_specs, check_vma=False
    )
```

profile of v0, /device:TPU:2, one launch (start us, length us, event | category | flops | bytes accessed | tf_op | source)
XLA Modules:
  0.0 325.1 jit_solution(17238749150550705226)
XLA Ops:
  8.1 3.3 %copy.101 = bf16[512,2048]{1,0:T(8,128)(2,1)} copy(bf16[512,2048]{1,0:T(8,128)(2,1)} %param.27) | data formatting | bytes 4194304
  12.2 2.6 convolution_convert_fusion
  14.8 2.5 reshape.190
  18.9 3.3 %fusion.122 = (f32[2,4,256]{2,1,0:T(4,128)S(1)}, f32[2,4,256,256]{2,3,1,0:T(8,128)}) fusion(pred[2,256]{1,0:T(4,128)(4,1)S(1)} %iota_compare_fusion, bf16[2,256,1,4,80]{1,0,4,3,2:T(2,128)(2,1)} %get-tuple-element.18, bf16[2,256,1,4,80]{1,0,4,3,2:T(2,128)(2,1)} %get-tuple-element.17), kind=kOutput, calls=%fused_computation.164 | convolution fusion | flops 85983488 | bytes 2761216 | tf_op jit(solution)/shard_map/sub | solution.py:113
  25.0 3.6 %fusion.73 = f32[128,4,1280]{2,0,1:T(8,128)} fusion(bf16[320,1280]{1,0:T(8,128)(2,1)} %param.20, bf16[128,4,320]{2,1,0:T(4,128)(2,1)S(1)} %dot_general.23), kind=kOutput, calls=%fused_computation.91 | convolution fusion | flops 419430400 | bytes 3768320 | tf_op jit(solution)/shard_map/dot_general | solution.py:118
  30.4 3.5 %reshape.188 = bf16[128,4,1280]{2,1,0:T(4,128)(2,1)} reshape(bf16[512,1280]{1,0:T(8,128)(2,1)} %param.16) | data formatting | bytes 2621440 | tf_op jit(solution)/shard_map/reshape | solution.py:121
  35.9 69.9 %reduce-scatter.2.cloned.1.call-done = f32[128,1,1280]{2,0,1:T(8,128)} async-done(((f32[128,4,1280]{2,0,1:T(8,128)}), f32[128,1,1280]{2,0,1:T(8,128)}) %reduce-scatter.2.cloned.1.call-update) | async-done | bytes 655376 | tf_op jit(solution)/shard_map/reduce_scatter | solution.py:123
  107.7 19.0 %all_to_all.30 = bf16[4,128,1280]{2,1,0:T(8,128)(2,1)} all-to-all(bf16[4,128,1280]{2,1,0:T(8,128)(2,1)S(1)} %broadcast_in_dim.30), channel_id=1, replica_groups=mesh['section'=16,'dp'=4,'mp'=4] {'dp'}, dimensions={0} | all-to-all | bytes 2621440 | tf_op jit(solution)/shard_map/all_to_all | solution.py:34
  126.7 3.4 %all-gather.2.cloned.1.call-done = bf16[1280,3329]{1,0:T(8,128)(2,1)} async-done(((bf16[80,3329]{1,0:T(8,128)(2,1)}), bf16[1280,3329]{1,0:T(8,128)(2,1)}) %all-gather.2.cloned.1.call-update) | async-done | bytes 8522256 | tf_op jit(solution)/shard_map/all_gather | solution.py:16
  130.1 5.3 %fusion.10 = bf16[512,1280]{1,0:T(8,128)(2,1)} fusion(bf16[512,1280]{1,0:T(8,128)(2,1)} %bitcast.62, bf16[1280,3329]{1,0:T(8,128)(2,1)} %all-gather.2.cloned.1.call-done), kind=kOutput, calls=%fused_computation.19 | convolution fusion | flops 1678376960 | bytes 5898240 | tf_op jit(solution)/shard_map/dot_general | solution.py:131
  136.6 73.0 %all-reduce.2.cloned.1.call-done = bf16[512,1280]{1,0:T(8,128)(2,1)} async-done(((bf16[512,1280]{1,0:T(8,128)(2,1)}), bf16[512,1280]{1,0:T(8,128)(2,1)}) %all-reduce.2.cloned.1.call-update) | async-done | bytes 1310736 | tf_op jit(solution)/shard_map/psum | solution.py:134
  209.6 12.3 %fusion.13 = bf16[512,2048]{1,0:T(8,128)(2,1)} fusion(bf16[1280,3329]{1,0:T(8,128)(2,1)} %all-gather.2.cloned.1.call-done, bf16[512,1280]{1,0:T(8,128)(2,1)} %all-reduce.2.cloned.1.call-done, f32[1280]{0:T(1024)S(1)} %convert_reduce_fusion.3), kind=kOutput, calls=%fused_computation.20 | convolution fusion | flops 2729312256 | bytes 8655872 | tf_op jit(solution)/shard_map/dot_general | solution.py:139
  221.9 5.1 %all-to-all-start.2 = ((bf16[4,128,2048]{2,1,0:T(8,128)(2,1)}), bf16[4,128,2048]{2,1,0:T(8,128)(2,1)}, u32[]{:S(2)}, u32[]{:S(2)}) async-start(bf16[4,128,2048]{2,1,0:T(8,128)(2,1)} %bitcast.61), calls=%async_computation.3 | async-start | bytes 4194304 | tf_op jit(solution)/shard_map/all_to_all | solution.py:48
  227.1 2.9 collective-permute-start
  233.5 18.9 %all-to-all-done.2 = bf16[4,128,2048]{2,1,0:T(8,128)(2,1)} async-done(((bf16[4,128,2048]{2,1,0:T(8,128)(2,1)}), bf16[4,128,2048]{2,1,0:T(8,128)(2,1)}, u32[]{:S(2)}, u32[]{:S(2)}) %all-to-all-start.2) | async-done | bytes 2097184 | tf_op jit(solution)/shard_map/all_to_all | solution.py:48
  252.4 6.9 %all-to-all-start = ((s32[64,1,2]{2,1,0:T(1,128)}), s32[64,1,2]{2,1,0:T(1,128)S(1)}, u32[]{:S(2)}, u32[]{:S(2)}) async-start(s32[64,1,2]{2,1,0:T(1,128)} %bitcast.15), calls=%async_computation | async-start | bytes 65536 | tf_op jit(solution)/shard_map/all_to_all | solution.py:162
  265.6 8.0 %scatter_fusion = bf16[64,2,2048]{2,1,0:T(2,128)(2,1)} fusion(bf16[64,2,2048]{2,1,0:T(2,128)(2,1)} %broadcast_in_dim.24, s32[64]{0:T(128)S(1)} %fusion.83, bf16[64,2,2048]{2,1,0:T(2,128)(2,1)S(1)} %add_convert_fusion), kind=kCustom, calls=%fused_computation.1 | custom fusion | bytes 1573120 | tf_op jit(solution)/shard_map/scatter | solution.py:153
  273.6 8.8 %all-to-all-start.3 = ((bf16[64,2,2048]{2,1,0:T(2,128)(2,1)}), bf16[64,2,2048]{2,1,0:T(2,128)(2,1)S(1)}, u32[]{:S(2)}, u32[]{:S(2)}) async-start(bf16[64,2,2048]{2,1,0:T(2,128)(2,1)} %scatter_fusion), calls=%async_computation.4 | async-start | bytes 1048576 | tf_op jit(solution)/shard_map/all_to_all | solution.py:161
  283.8 10.3 %all-to-all-done.3 = bf16[64,2,2048]{2,1,0:T(2,128)(2,1)S(1)} async-done(((bf16[64,2,2048]{2,1,0:T(2,128)(2,1)}), bf16[64,2,2048]{2,1,0:T(2,128)(2,1)S(1)}, u32[]{:S(2)}, u32[]{:S(2)}) %all-to-all-start.3) | async-done | bytes 524320 | tf_op jit(solution)/shard_map/all_to_all | solution.py:161
  294.3 4.6 %scatter_fusion.1 = bf16[512,2048]{1,0:T(8,128)(2,1)} fusion(bf16[512,2048]{1,0:T(8,128)(2,1)} %copy.101, s32[128]{0:T(128)S(1)} %fusion.87, bf16[128,2048]{1,0:T(8,128)(2,1)S(1)} %reshape.225), kind=kCustom, calls=%fused_computation.2 | custom fusion | bytes 1573376 | tf_op jit(solution)/shard_map/scatter | solution.py:164
  298.9 2.4 fusion.3
  301.9 3.9 %all-to-all-start.4 = ((f32[4,1,512]{2,1,0:T(1,128)}), f32[4,1,512]{2,1,0:T(1,128)S(1)}, u32[]{:S(2)}, u32[]{:S(2)}) async-start(f32[4,1,512]{2,1,0:T(1,128)} %broadcast_in_dim.31), calls=%async_computation.5 | async-start | bytes 16384 | tf_op jit(solution)/shard_map/all_to_all | solution.py:34
  305.8 7.7 %all-to-all-done.4 = f32[4,1,512]{2,1,0:T(1,128)S(1)} async-done(((f32[4,1,512]{2,1,0:T(1,128)}), f32[4,1,512]{2,1,0:T(1,128)S(1)}, u32[]{:S(2)}, u32[]{:S(2)}) %all-to-all-start.4) | async-done | bytes 8224 | tf_op jit(solution)/shard_map/all_to_all | solution.py:34
  313.5 4.1 %fusion.5 = bf16[512,2048]{1,0:T(8,128)(2,1)} fusion(f32[2048]{0:T(1024)S(1)} %convert_element_type.105, f32[512]{0:T(512)S(1)} %add_rsqrt_fusion, bf16[512,2048]{1,0:T(8,128)(2,1)} %scatter_fusion.1, bf16[512,2048]{1,0:T(8,128)(2,1)} %collective-permute-done, pred[]{:T(512)S(6)} %eq.6), kind=kLoop, calls=%fused_computation.10 | loop fusion | flops 5242880 | bytes 6301697 | tf_op jit(solution)/shard_map/convert_element_type | solution.py:174
  (75 shorter events, 24.0 us)
Async XLA Ops:
  8.0 4.2 %copy-start = (bf16[1280,3,320]{0,2,1:T(8,128)(2,1)S(1)}, bf16[1280,3,320]{0,2,1:T(8,128)(2,1)}, u32[]{:S(2)}) copy-start(bf16[1280,3,320]{0,2,1:T(8,128)(2,1)} %param.19) | copy-start | bytes 7372804
  8.0 4.1 %copy-start.5 = (bf16[1280]{0:T(1024)(128)(2,1)S(1)}, bf16[1280]{0:T(1024)(128)(2,1)}, u32[]{:S(2)}) copy-start(bf16[1280]{0:T(1024)(128)(2,1)} %param.21) | copy-start | bytes 7684
  8.0 97.8 %reduce-scatter.2.cloned.1.call-start = ((), (), s32[]{:S(2)}) async-start(), calls=%async_computation.6 | async-start | bytes 3276800 | tf_op jit(solution)/shard_map/reduce_scatter | solution.py:123
  8.1 3.3 %copy-start.1 = (bf16[512,1280]{1,0:T(8,128)(2,1)S(1)}, bf16[512,1280]{1,0:T(8,128)(2,1)}, u32[]{:S(2)}) copy-start(bf16[512,1280]{1,0:T(8,128)(2,1)} %param.16) | copy-start | bytes 3932164
  14.8 4.1 %copy-start.9 = (s32[2]{0:T(128)S(1)}, s32[2]{0:T(128)}, u32[]{:S(2)}) copy-start(s32[2]{0:T(128)} %param.17) | copy-start | bytes 28
  18.9 3.4 %copy-start.3 = (bf16[2,256,1,4,80]{1,0,4,3,2:T(2,128)(2,1)S(1)}, bf16[2,256,1,4,80]{1,0,4,3,2:T(2,128)(2,1)}, u32[]{:S(2)}) copy-start(bf16[2,256,1,4,80]{1,0,4,3,2:T(2,128)(2,1)} %get-tuple-element.16) | copy-start | bytes 983044
  24.9 3.7 %copy-start.12 = (bf16[80]{0:T(256)(128)(2,1)S(1)}, bf16[80]{0:T(256)(128)(2,1)}, u32[]{:S(2)}) copy-start(bf16[80]{0:T(256)(128)(2,1)} %param.24) | copy-start | bytes 484
  25.0 3.8 %copy-start.2 = (bf16[80,2048]{1,0:T(8,128)(2,1)S(1)}, bf16[80,2048]{1,0:T(8,128)(2,1)}, u32[]{:S(2)}) copy-start(bf16[80,2048]{1,0:T(8,128)(2,1)} %param.25) | copy-start | bytes 983044
  28.6 0.9 copy-start.4
  28.6 5.3 %copy-start.6 = (bf16[1280]{0:T(1024)(128)(2,1)S(1)}, bf16[1280]{0:T(1024)(128)(2,1)}, u32[]{:S(2)}) copy-start(bf16[1280]{0:T(1024)(128)(2,1)} %param.22) | copy-start | bytes 7684
  28.6 101.5 %all-gather.2.cloned.1.call-start = ((), (), s32[]{:S(2)}) async-start(), calls=%async_computation.7 | async-start | bytes 9400320 | tf_op jit(solution)/shard_map/all_gather | solution.py:16
  30.4 179.2 %all-reduce.2.cloned.1.call-start = ((), (), s32[]{:S(2)}) async-start(), calls=%async_computation.8 | async-start | bytes 2621440 | tf_op jit(solution)/shard_map/psum | solution.py:134
  221.9 8.6 %copy-start.7 = (bf16[2048]{0:T(1024)(128)(2,1)S(1)}, bf16[2048]{0:T(1024)(128)(2,1)}, u32[]{:S(2)}) copy-start(bf16[2048]{0:T(1024)(128)(2,1)} %param.26) | copy-start | bytes 12292
  221.9 8.6 %copy-start.10 = (s32[128]{0:T(128)S(1)}, s32[128]{0:T(128)}, u32[]{:S(2)}) copy-start(s32[128]{0:T(128)} %param.18) | copy-start | bytes 1540
  221.9 8.6 %copy-start.11 = (pred[128]{0:T(512)(128)(4,1)S(1)}, pred[128]{0:T(512)(128)(4,1)}, u32[]{:S(2)}) copy-start(pred[128]{0:T(512)(128)(4,1)} %constant.225) | copy-start | bytes 388
  221.9 30.5 %all-to-all-start.2 = ((bf16[4,128,2048]{2,1,0:T(8,128)(2,1)}), bf16[4,128,2048]{2,1,0:T(8,128)(2,1)}, u32[]{:S(2)}, u32[]{:S(2)}) async-start(bf16[4,128,2048]{2,1,0:T(8,128)(2,1)} %bitcast.61), calls=%async_computation.3 | async-start | bytes 4194304 | tf_op jit(solution)/shard_map/all_to_all | solution.py:48
  227.1 71.9 %collective-permute-start = (bf16[512,2048]{1,0:T(8,128)(2,1)}, bf16[512,2048]{1,0:T(8,128)(2,1)}, u32[]{:S(2)}, u32[]{:S(2)}) collective-permute-start(bf16[512,2048]{1,0:T(8,128)(2,1)} %param.28), channel_id=1, source_target_pairs={{0,16},{16,32},{32,48},{48,64},{64,80},{80,96},{96,112},{112,128},... | collective-permute-start | bytes 6291464 | tf_op jit(solution)/shard_map/ppermute | solution.py:55
  252.4 21.2 %all-to-all-start = ((s32[64,1,2]{2,1,0:T(1,128)}), s32[64,1,2]{2,1,0:T(1,128)S(1)}, u32[]{:S(2)}, u32[]{:S(2)}) async-start(s32[64,1,2]{2,1,0:T(1,128)} %bitcast.15), calls=%async_computation | async-start | bytes 65536 | tf_op jit(solution)/shard_map/all_to_all | solution.py:162
  273.6 20.5 %all-to-all-start.3 = ((bf16[64,2,2048]{2,1,0:T(2,128)(2,1)}), bf16[64,2,2048]{2,1,0:T(2,128)(2,1)S(1)}, u32[]{:S(2)}, u32[]{:S(2)}) async-start(bf16[64,2,2048]{2,1,0:T(2,128)(2,1)} %scatter_fusion), calls=%async_computation.4 | async-start | bytes 1048576 | tf_op jit(solution)/shard_map/all_to_all | solution.py:161
  298.9 6.8 %copy-start.8 = (bf16[2048]{0:T(1024)(128)(2,1)S(1)}, bf16[2048]{0:T(1024)(128)(2,1)}, u32[]{:S(2)}) copy-start(bf16[2048]{0:T(1024)(128)(2,1)} %param.29) | copy-start | bytes 12292
  301.9 11.6 %all-to-all-start.4 = ((f32[4,1,512]{2,1,0:T(1,128)}), f32[4,1,512]{2,1,0:T(1,128)S(1)}, u32[]{:S(2)}, u32[]{:S(2)}) async-start(f32[4,1,512]{2,1,0:T(1,128)} %broadcast_in_dim.31), calls=%async_computation.5 | async-start | bytes 16384 | tf_op jit(solution)/shard_map/all_to_all | solution.py:34
Sparse Core Ops, SparseCore 0:
  28.7 77.1 reduce-scatter.1
  135.5 73.9 all-reduce.1
Sparse Core Ops, SparseCore 1:
  30.9 99.1 all-gather.1
where the time goes:
time: 326 us; the launch traced here: 325 us
  waiting for transfers between devices  183 us (56%)
  local copies, waits for them, and re-layouts  33.5 us (10%)
  matrix products  29 us (9%)
  starting transfers between devices  27.7 us (8%)
  blocking collectives  19 us (6%)
  other arithmetic  16.8 us (5%)
  between operations  15.7 us (5%)
    psum x1, waiting for transfers between devices, per_device(): lax.psum(first_partial.astype(jnp.bfloat16), 'mp').astype(jnp.float32)  73 us
    reduce_scatter x1, waiting for transfers between devices, per_device(): lax.psum_scatter(partial_proj.reshape(merged_rows, 4, width), 'mp', scatt...  69.9 us
    all_to_all x1, blocking collectives, copy_for_each(): return lax.all_to_all(copies, axis, split_axis=0, concat_axis=0, tiled=True)  19 us
    all_to_all x1, waiting for transfers between devices, sent_and_summed(): lax.all_to_all(cut_along(value, dim, devices), axis, 0, 0, tiled=True)  18.9 us
    dot_general x1, matrix products, per_device(): jnp.dot(hidden, second_full, preferred_element_type=jnp.float32)  12.3 us
    all_to_all x1, waiting for transfers between devices, per_device(): lax.all_to_all(send_rows, ('section', 'dp'), split_axis=0, concat_axis=0,...  10.3 us
    all_to_all x1, starting transfers between devices, per_device(): lax.all_to_all(send_rows, ('section', 'dp'), split_axis=0, concat_axis=0,...  8.83 us
    scatter x1, local copies, waits for them, and re-layouts, per_device(): send_rows = jnp.zeros((group_count, run_cap, feature_cols), jnp.bfloat16)...  7.99 us
  transfers between devices with their start and end apart: 8, of which 6 were waited for; matrix products, arithmetic and copies ran while one was open for 10% of the time, Pallas kernels for 0%

commit v1 on v0

--- a/solution.py
+++ b/solution.py
@@ -131,7 +131,9 @@
     first_partial = jnp.dot(
         gathered_copies(merge_part, "dp", 0), first_full, preferred_element_type=jnp.float32
     )
-    first_total = lax.psum(first_partial.astype(jnp.bfloat16), "mp").astype(jnp.float32)
+    first_total = jnp.sum(lax.all_gather(first_partial.astype(jnp.bfloat16), "mp"), axis=0).astype(
+        jnp.float32
+    )
     hidden = jax.nn.gelu(first_total + bias_full.astype(jnp.float32), approximate=False).astype(
         jnp.bfloat16
     )

time: 326 us -> 361 us (1.11)
  waiting for transfers between devices: 183 us -> 202 us
  starting transfers between devices: 27.7 us -> 39 us
  other arithmetic: 16.8 us -> 21.5 us
    all_gather x0 -> x1, waiting for transfers between devices: none -> 92 us  [per_device(): lax.all_gather(first_partial.astype(jnp.bfloat16), 'mp')]
    psum x1 -> x0, waiting for transfers between devices: 73 us -> none  [per_device(): lax.psum(first_partial.astype(jnp.bfloat16), 'mp').astype(jnp.float32)]
    all_to_all x1, starting transfers between devices: 6.87 us -> 19 us  [per_device(): lax.all_to_all(send_place, ('section', 'dp'), split_axis=0, concat_axis=0...]
    reduce_sum x0 -> x1, other arithmetic: none -> 4.69 us  [per_device(): jnp.sum(lax.all_gather(first_partial.astype(jnp.bfloat16), 'mp'), axis=0)]
  transfers between devices with their start and end apart: 8 -> 8, of which waited for: 6 -> 6; matrix products, arithmetic and copies ran while one was open for 10% -> 9% of each run, Pallas kernels for 0% -> 0%
where the time goes in v1:
time: 361 us; the launch traced here: 360 us
  waiting for transfers between devices  202 us (56%)
  starting transfers between devices  39 us (11%)
  local copies, waits for them, and re-layouts  33.5 us (9%)
  matrix products  29 us (8%)
  other arithmetic  21.5 us (6%)
  blocking collectives  19 us (5%)
  between operations  15.8 us (4%)
    all_gather x1, waiting for transfers between devices, per_device(): lax.all_gather(first_partial.astype(jnp.bfloat16), 'mp')  92 us
    reduce_scatter x1, waiting for transfers between devices, per_device(): lax.psum_scatter(partial_proj.reshape(merged_rows, 4, width), 'mp', scatt...  69.9 us
    all_to_all x1, blocking collectives, copy_for_each(): return lax.all_to_all(copies, axis, split_axis=0, concat_axis=0, tiled=True)  19 us
    all_to_all x1, starting transfers between devices, per_device(): lax.all_to_all(send_place, ('section', 'dp'), split_axis=0, concat_axis=0...  19 us
    all_to_all x1, waiting for transfers between devices, sent_and_summed(): lax.all_to_all(cut_along(value, dim, devices), axis, 0, 0, tiled=True)  18.9 us
    dot_general x1, matrix products, per_device(): jnp.dot(hidden, second_full, preferred_element_type=jnp.float32)  12.3 us
    all_to_all x1, waiting for transfers between devices, per_device(): lax.all_to_all(send_rows, ('section', 'dp'), split_axis=0, concat_axis=0,...  10.3 us
    all_to_all x1, starting transfers between devices, per_device(): lax.all_to_all(send_rows, ('section', 'dp'), split_axis=0, concat_axis=0,...  8.83 us
  transfers between devices with their start and end apart: 8, of which 6 were waited for; matrix products, arithmetic and copies ran while one was open for 9% of the time, Pallas kernels for 0%

profile of v1, /device:TPU:2, one launch (start us, length us, event | category | flops | bytes accessed | tf_op | source)
XLA Modules:
  0.0 360.0 jit_solution(5437647798026712291)
XLA Ops:
  8.1 3.3 copy.100
  12.2 2.6 convolution_convert_fusion
  14.8 2.5 reshape.190
  18.9 3.3 fusion.122
  25.0 3.6 %fusion.73 = f32[128,4,1280]{2,0,1:T(8,128)} fusion(bf16[320,1280]{1,0:T(8,128)(2,1)} %param.20, bf16[128,4,320]{2,1,0:T(4,128)(2,1)S(1)} %dot_general.23), kind=kOutput, calls=%fused_computation.91 | convolution fusion | flops 419430400 | bytes 3768320 | tf_op jit(solution)/shard_map/dot_general | solution.py:118
  30.4 3.5 reshape.188
  35.9 69.9 %reduce-scatter.2.cloned.1.call-done = f32[128,1,1280]{2,0,1:T(8,128)} async-done(((f32[128,4,1280]{2,0,1:T(8,128)}), f32[128,1,1280]{2,0,1:T(8,128)}) %reduce-scatter.2.cloned.1.call-update) | async-done | bytes 655376 | tf_op jit(solution)/shard_map/reduce_scatter | solution.py:123
  107.7 19.0 %all_to_all.30 = bf16[4,128,1280]{2,1,0:T(8,128)(2,1)} all-to-all(bf16[4,128,1280]{2,1,0:T(8,128)(2,1)S(1)} %broadcast_in_dim.30), channel_id=1, replica_groups=mesh['section'=16,'dp'=4,'mp'=4] {'dp'}, dimensions={0} | all-to-all | bytes 2621440 | tf_op jit(solution)/shard_map/all_to_all | solution.py:34
  126.7 3.4 all-gather.4.cloned.1.call-done
  130.1 5.3 %fusion.10 = bf16[512,1280]{1,0:T(8,128)(2,1)} fusion(bf16[512,1280]{1,0:T(8,128)(2,1)} %bitcast.64, bf16[1280,3329]{1,0:T(8,128)(2,1)} %all-gather.4.cloned.1.call-done), kind=kOutput, calls=%fused_computation.19 | convolution fusion | flops 1678376960 | bytes 5898240 | tf_op jit(solution)/shard_map/dot_general | solution.py:131
  136.6 92.0 %all-gather.6.cloned.1.call-done = bf16[2048,1280]{1,0:T(8,128)(2,1)} async-done(((bf16[512,1280]{1,0:T(8,128)(2,1)}), bf16[2048,1280]{1,0:T(8,128)(2,1)}) %all-gather.6.cloned.1.call-update) | async-done | bytes 5242896 | tf_op jit(solution)/shard_map/all_gather | solution.py:134
  228.6 4.7 %reduce_sum.91 = bf16[512,1280]{1,0:T(8,128)(2,1)} reduce(bf16[4,512,1280]{2,1,0:T(8,128)(2,1)} %bitcast.62, bf16[]{:T(256)} %constant.179.clone.1), dimensions={0}, to_apply=%region_8.9 | reduce | flops 1966080 | bytes 6553602 | tf_op jit(solution)/shard_map/reduce_sum | solution.py:134
  233.3 12.3 %fusion.13 = bf16[512,2048]{1,0:T(8,128)(2,1)} fusion(bf16[1280,3329]{1,0:T(8,128)(2,1)} %all-gather.4.cloned.1.call-done, bf16[512,1280]{1,0:T(8,128)(2,1)} %reduce_sum.91, f32[1280]{0:T(1024)S(1)} %convert_reduce_fusion.3), kind=kOutput, calls=%fused_computation.20 | convolution fusion | flops 2729312256 | bytes 8655872 | tf_op jit(solution)/shard_map/dot_general | solution.py:141
  245.6 5.2 %all-to-all-start.2 = ((bf16[4,128,2048]{2,1,0:T(8,128)(2,1)}), bf16[4,128,2048]{2,1,0:T(8,128)(2,1)}, u32[]{:S(2)}, u32[]{:S(2)}) async-start(bf16[4,128,2048]{2,1,0:T(8,128)(2,1)} %bitcast.63), calls=%async_computation.3 | async-start | bytes 4194304 | tf_op jit(solution)/shard_map/all_to_all | solution.py:48
  250.8 2.6 collective-permute-start
  257.0 18.9 %all-to-all-done.2 = bf16[4,128,2048]{2,1,0:T(8,128)(2,1)} async-done(((bf16[4,128,2048]{2,1,0:T(8,128)(2,1)}), bf16[4,128,2048]{2,1,0:T(8,128)(2,1)}, u32[]{:S(2)}, u32[]{:S(2)}) %all-to-all-start.2) | async-done | bytes 2097184 | tf_op jit(solution)/shard_map/all_to_all | solution.py:48
  275.9 19.0 %all-to-all-start = ((s32[64,1,2]{2,1,0:T(1,128)}), s32[64,1,2]{2,1,0:T(1,128)S(1)}, u32[]{:S(2)}, u32[]{:S(2)}) async-start(s32[64,1,2]{2,1,0:T(1,128)} %bitcast.16), calls=%async_computation | async-start | bytes 65536 | tf_op jit(solution)/shard_map/all_to_all | solution.py:164
  301.2 8.0 %scatter_fusion = bf16[64,2,2048]{2,1,0:T(2,128)(2,1)} fusion(bf16[64,2,2048]{2,1,0:T(2,128)(2,1)} %broadcast_in_dim.24, s32[64]{0:T(128)S(1)} %fusion.83, bf16[64,2,2048]{2,1,0:T(2,128)(2,1)S(1)} %add_convert_fusion), kind=kCustom, calls=%fused_computation.1 | custom fusion | bytes 1573120 | tf_op jit(solution)/shard_map/scatter | solution.py:155
  309.2 8.8 %all-to-all-start.3 = ((bf16[64,2,2048]{2,1,0:T(2,128)(2,1)}), bf16[64,2,2048]{2,1,0:T(2,128)(2,1)S(1)}, u32[]{:S(2)}, u32[]{:S(2)}) async-start(bf16[64,2,2048]{2,1,0:T(2,128)(2,1)} %scatter_fusion), calls=%async_computation.4 | async-start | bytes 1048576 | tf_op jit(solution)/shard_map/all_to_all | solution.py:163
  319.4 10.3 %all-to-all-done.3 = bf16[64,2,2048]{2,1,0:T(2,128)(2,1)S(1)} async-done(((bf16[64,2,2048]{2,1,0:T(2,128)(2,1)}), bf16[64,2,2048]{2,1,0:T(2,128)(2,1)S(1)}, u32[]{:S(2)}, u32[]{:S(2)}) %all-to-all-start.3) | async-done | bytes 524320 | tf_op jit(solution)/shard_map/all_to_all | solution.py:163
  329.9 4.6 %scatter_fusion.1 = bf16[512,2048]{1,0:T(8,128)(2,1)} fusion(bf16[512,2048]{1,0:T(8,128)(2,1)} %copy.100, s32[128]{0:T(128)S(1)} %fusion.87, bf16[128,2048]{1,0:T(8,128)(2,1)S(1)} %reshape.225), kind=kCustom, calls=%fused_computation.2 | custom fusion | bytes 1573376 | tf_op jit(solution)/shard_map/scatter | solution.py:166
  337.5 3.2 all-to-all-start.4
  340.7 7.7 %all-to-all-done.4 = f32[4,1,512]{2,1,0:T(1,128)S(1)} async-done(((f32[4,1,512]{2,1,0:T(1,128)}), f32[4,1,512]{2,1,0:T(1,128)S(1)}, u32[]{:S(2)}, u32[]{:S(2)}) %all-to-all-start.4) | async-done | bytes 8224 | tf_op jit(solution)/shard_map/all_to_all | solution.py:34
  348.4 4.1 %fusion.5 = bf16[512,2048]{1,0:T(8,128)(2,1)} fusion(f32[2048]{0:T(1024)S(1)} %convert_element_type.107, f32[512]{0:T(512)S(1)} %add_rsqrt_fusion, bf16[512,2048]{1,0:T(8,128)(2,1)} %scatter_fusion.1, bf16[512,2048]{1,0:T(8,128)(2,1)} %collective-permute-done, pred[]{:T(512)S(6)} %eq.6), kind=kLoop, calls=%fused_computation.10 | loop fusion | flops 5242880 | bytes 6301697 | tf_op jit(solution)/shard_map/convert_element_type | solution.py:176
  (76 shorter events, 26.4 us)
Async XLA Ops:
  8.0 4.2 %copy-start = (bf16[1280,3,320]{0,2,1:T(8,128)(2,1)S(1)}, bf16[1280,3,320]{0,2,1:T(8,128)(2,1)}, u32[]{:S(2)}) copy-start(bf16[1280,3,320]{0,2,1:T(8,128)(2,1)} %param.19) | copy-start | bytes 7372804
  8.0 4.1 %copy-start.5 = (bf16[1280]{0:T(1024)(128)(2,1)S(1)}, bf16[1280]{0:T(1024)(128)(2,1)}, u32[]{:S(2)}) copy-start(bf16[1280]{0:T(1024)(128)(2,1)} %param.21) | copy-start | bytes 7684
  8.0 97.8 %reduce-scatter.2.cloned.1.call-start = ((), (), s32[]{:S(2)}) async-start(), calls=%async_computation.6 | async-start | bytes 3276800 | tf_op jit(solution)/shard_map/reduce_scatter | solution.py:123
  8.1 3.3 copy-start.1
  14.8 4.1 %copy-start.9 = (s32[2]{0:T(128)S(1)}, s32[2]{0:T(128)}, u32[]{:S(2)}) copy-start(s32[2]{0:T(128)} %param.17) | copy-start | bytes 28
  18.9 3.4 copy-start.3
  24.9 3.7 %copy-start.12 = (bf16[80]{0:T(256)(128)(2,1)S(1)}, bf16[80]{0:T(256)(128)(2,1)}, u32[]{:S(2)}) copy-start(bf16[80]{0:T(256)(128)(2,1)} %param.24) | copy-start | bytes 484
  25.0 3.8 %copy-start.2 = (bf16[80,2048]{1,0:T(8,128)(2,1)S(1)}, bf16[80,2048]{1,0:T(8,128)(2,1)}, u32[]{:S(2)}) copy-start(bf16[80,2048]{1,0:T(8,128)(2,1)} %param.25) | copy-start | bytes 983044
  28.6 0.9 copy-start.4
  28.6 5.3 %copy-start.6 = (bf16[1280]{0:T(1024)(128)(2,1)S(1)}, bf16[1280]{0:T(1024)(128)(2,1)}, u32[]{:S(2)}) copy-start(bf16[1280]{0:T(1024)(128)(2,1)} %param.22) | copy-start | bytes 7684
  28.6 101.5 %all-gather.4.cloned.1.call-start = ((), (), s32[]{:S(2)}) async-start(), calls=%async_computation.7 | async-start | bytes 9400320 | tf_op jit(solution)/shard_map/all_gather | solution.py:16
  30.4 198.2 %all-gather.6.cloned.1.call-start = ((), (), s32[]{:S(2)}) async-start(), calls=%async_computation.8 | async-start | bytes 6553600 | tf_op jit(solution)/shard_map/all_gather | solution.py:134
  245.6 8.4 %copy-start.7 = (bf16[2048]{0:T(1024)(128)(2,1)S(1)}, bf16[2048]{0:T(1024)(128)(2,1)}, u32[]{:S(2)}) copy-start(bf16[2048]{0:T(1024)(128)(2,1)} %param.26) | copy-start | bytes 12292
  245.6 8.4 %copy-start.10 = (s32[128]{0:T(128)S(1)}, s32[128]{0:T(128)}, u32[]{:S(2)}) copy-start(s32[128]{0:T(128)} %param.18) | copy-start | bytes 1540
  245.6 8.4 %copy-start.11 = (pred[128]{0:T(512)(128)(4,1)S(1)}, pred[128]{0:T(512)(128)(4,1)}, u32[]{:S(2)}) copy-start(pred[128]{0:T(512)(128)(4,1)} %constant.226) | copy-start | bytes 388
  245.6 30.2 %all-to-all-start.2 = ((bf16[4,128,2048]{2,1,0:T(8,128)(2,1)}), bf16[4,128,2048]{2,1,0:T(8,128)(2,1)}, u32[]{:S(2)}, u32[]{:S(2)}) async-start(bf16[4,128,2048]{2,1,0:T(8,128)(2,1)} %bitcast.63), calls=%async_computation.3 | async-start | bytes 4194304 | tf_op jit(solution)/shard_map/all_to_all | solution.py:48
  250.8 83.7 %collective-permute-start = (bf16[512,2048]{1,0:T(8,128)(2,1)}, bf16[512,2048]{1,0:T(8,128)(2,1)}, u32[]{:S(2)}, u32[]{:S(2)}) collective-permute-start(bf16[512,2048]{1,0:T(8,128)(2,1)} %param.28), channel_id=1, source_target_pairs={{0,16},{16,32},{32,48},{48,64},{64,80},{80,96},{96,112},{112,128},... | collective-permute-start | bytes 6291464 | tf_op jit(solution)/shard_map/ppermute | solution.py:55
  275.9 33.3 %all-to-all-start = ((s32[64,1,2]{2,1,0:T(1,128)}), s32[64,1,2]{2,1,0:T(1,128)S(1)}, u32[]{:S(2)}, u32[]{:S(2)}) async-start(s32[64,1,2]{2,1,0:T(1,128)} %bitcast.16), calls=%async_computation | async-start | bytes 65536 | tf_op jit(solution)/shard_map/all_to_all | solution.py:164
  309.2 20.5 %all-to-all-start.3 = ((bf16[64,2,2048]{2,1,0:T(2,128)(2,1)}), bf16[64,2,2048]{2,1,0:T(2,128)(2,1)S(1)}, u32[]{:S(2)}, u32[]{:S(2)}) async-start(bf16[64,2,2048]{2,1,0:T(2,128)(2,1)} %scatter_fusion), calls=%async_computation.4 | async-start | bytes 1048576 | tf_op jit(solution)/shard_map/all_to_all | solution.py:163
  334.5 6.2 %copy-start.8 = (bf16[2048]{0:T(1024)(128)(2,1)S(1)}, bf16[2048]{0:T(1024)(128)(2,1)}, u32[]{:S(2)}) copy-start(bf16[2048]{0:T(1024)(128)(2,1)} %param.29) | copy-start | bytes 12292
  337.5 11.0 %all-to-all-start.4 = ((f32[4,1,512]{2,1,0:T(1,128)}), f32[4,1,512]{2,1,0:T(1,128)S(1)}, u32[]{:S(2)}, u32[]{:S(2)}) async-start(f32[4,1,512]{2,1,0:T(1,128)} %broadcast_in_dim.31), calls=%async_computation.5 | async-start | bytes 16384 | tf_op jit(solution)/shard_map/all_to_all | solution.py:34
Sparse Core Ops, SparseCore 0:
  28.7 77.1 reduce-scatter.1
  135.5 92.9 all-gather.5
Sparse Core Ops, SparseCore 1:
  30.9 99.1 all-gather.3
